TPU v7x, 32 devices: a whole 2x2x4 slice. The times are simulated.
32 devices in a mesh: dp: 4 (over x, core), mp: 8 (over z, y).
Axes of the slice: x: 2, y: 2, z: 4, core: 2. Of those that a mesh axis runs over, the one named last changes fastest.
Arguments:
- tokens: bfloat16 [1024, 8192], P('dp'), may hold values from -6 to 6
- norm_gain: float32 [8192], replicated, may hold values from 0.5 to 1.5
- gate_weight: bfloat16 [8192, 28672], P('dp', 'mp'), may hold values from -0.0625 to 0.0625
- gate_mask: int32 [8192, 896], P('dp', 'mp'), may hold values from -2147483648 to 2147483646
- up_weight: bfloat16 [8192, 28672], P('dp', 'mp'), may hold values from -0.0625 to 0.0625
- up_mask: int32 [8192, 896], P('dp', 'mp'), may hold values from -2147483648 to 2147483646
- down_weight: bfloat16 [28672, 8192], P('mp', 'dp'), may hold values from -0.03125 to 0.03125
- down_mask: int32 [28672, 256], P('mp', 'dp'), may hold values from -2147483648 to 2147483647, as said below
Outputs:
- mixed: bfloat16 [1024, 8192], P('mp', 'dp')
- input_norms: float32 [8192], P('dp')
- hidden_norms: float32 [28672], P('mp')
Inputs may be any that keep to these rules, and one draw needn't show every extreme that they name: `down_mask`: in every word each of the eight aligned groups of four bits holds exactly two ones, so exactly two of every four consecutive columns of the down projection are kept.
All inputs are finite; a program needn't handle non-finite values.
Results may differ from a plain program's by a relative error of at most 0.025.
Values may be sent and summed in bfloat16 or wider, within the bound.
A program may use at most 192 MiB of HBM per device.

v0:
```python
import jax
import jax.numpy as jnp
from jax import lax
from jax.sharding import PartitionSpec as P


def keep_entries(weight, packed):
    shifts = jnp.arange(32, dtype=jnp.int32)
    kept_bits = jnp.right_shift(packed[..., None], shifts) & 1
    kept_bits = kept_bits.reshape(weight.shape)
    return jnp.where(kept_bits == 1, weight, jnp.zeros_like(weight))


def on_device(
    tokens, norm_gain, gate_weight, gate_mask, up_weight, up_mask, down_weight, down_mask
):
    values = tokens.astype(jnp.float32)
    scale = lax.rsqrt(jnp.mean(values * values, axis=1, keepdims=True) + 1e-05)
    normed = (values * scale * norm_gain).astype(jnp.bfloat16)
    columns = lax.all_to_all(normed, "dp", split_axis=1, concat_axis=0, tiled=True)
    widened = columns.astype(jnp.float32)
    input_norms = jnp.sqrt(jnp.sum(widened * widened, axis=0))
    gate_kept = keep_entries(gate_weight, gate_mask)
    up_kept = keep_entries(up_weight, up_mask)
    down_kept = keep_entries(down_weight, down_mask)
    units = gate_kept.shape[1]
    gate_part = jnp.dot(columns, gate_kept, preferred_element_type=jnp.float32)
    up_part = jnp.dot(columns, up_kept, preferred_element_type=jnp.float32)
    both_sums = lax.psum_scatter(
        jnp.concatenate([gate_part, up_part], axis=1).astype(jnp.bfloat16),
        "dp",
        scatter_dimension=0,
        tiled=True,
    ).astype(jnp.float32)
    hidden = (jax.nn.silu(both_sums[:, :units]) * both_sums[:, units:]).astype(jnp.bfloat16)
    wide_hidden = hidden.astype(jnp.float32)
    squares = lax.psum(jnp.sum(wide_hidden * wide_hidden, axis=0), "dp")
    hidden_norms = jnp.sqrt(squares)
    partial_out = jnp.dot(
        lax.all_gather(hidden, "dp", axis=0, tiled=True),
        down_kept,
        preferred_element_type=jnp.float32,
    )
    mixed = lax.psum_scatter(
        partial_out.astype(jnp.bfloat16), "mp", scatter_dimension=0, tiled=True
    )
    return (mixed, input_norms, hidden_norms)


def solution(mesh):
    return jax.shard_map(
        on_device,
        mesh=mesh,
        in_specs=(
            P("dp", None),
            P(),
            P("dp", "mp"),
            P("dp", "mp"),
            P("dp", "mp"),
            P("dp", "mp"),
            P("mp", "dp"),
            P("mp", "dp"),
        ),
        out_specs=(P("mp", "dp"), P("dp"), P("mp")),
        check_vma=False,
    )
```

profile of v0, /device:TPU:0, one launch (start us, length us, event | category | flops | bytes accessed | tf_op | source)
XLA Modules:
  0.0 449.8 jit_solution(9891590436069383037)
XLA Ops:
  7.2 0.0 copy-start.4
  7.2 6.4 %copy.17 = bf16[256,8192]{0,1:T(8,128)(2,1)} copy(bf16[256,8192]{1,0:T(8,128)(2,1)} %param.8) | data formatting | bytes 8388608 | tf_op args[0]
  13.6 3.3 fusion.9
  16.9 0.0 copy-done.4
  16.9 4.2 fusion.11
  21.0 4.9 %all-to-all-start = ((bf16[256,4,2048]{0,2,1:T(8,128)(2,1)}), bf16[256,4,2048]{0,2,1:T(8,128)(2,1)}, u32[]{:S(2)}, u32[]{:S(2)}) async-start(bf16[256,4,2048]{0,2,1:T(8,128)(2,1)} %bitcast.34), calls=%async_computation | async-start | bytes 8388608 | tf_op jit(solution)/shard_map/all_to_all | solution.py:20
  25.9 0.0 reduce-scatter.3.cloned.1.call-start
  26.0 0.1 shift_right_arithmetic.63
  26.1 20.3 %copy.19 = bf16[2048,3584]{0,1:T(8,128)(2,1)} copy(bf16[2048,3584]{1,0:T(8,128)(2,1)} %param.10) | data formatting | bytes 29360128 | tf_op args[2]
  46.4 0.0 copy-start.1
  46.4 0.0 copy-start.2
  46.4 20.5 %copy.20 = bf16[2048,3584]{0,1:T(8,128)(2,1)} copy(bf16[2048,3584]{1,0:T(8,128)(2,1)} %param.12) | data formatting | bytes 29360128 | tf_op args[4]
  66.9 0.0 copy-done.1
  66.9 0.0 copy-done.2
  66.9 28.4 %fusion.6 = (bf16[2048,3584]{0,1:T(8,128)(2,1)}, bf16[2048,3584]{0,1:T(8,128)(2,1)}) fusion(bf16[2048,3584]{0,1:T(8,128)(2,1)} %copy.19, s32[3584]{0:T(1024)S(1)} %shift_right_arithmetic.63, s32[2048,112]{0,1:T(8,128)S(1)} %copy-done.1, bf16[2048,3584]{0,1:T(8,128)(2,1)} %copy.20, s32[2048,112]{0,1:T(8,128)S(1)} %copy-done.2), kind=kLoop, calls=%fused_computation.9 | loop fusion | flops 58720256 | bytes 60569600 | tf_op jit(solution)/shard_map/jit(_where)/select_n | solution.py:11
  95.3 0.0 all-to-all-done
  95.3 6.3 %copy.18 = bf16[4,256,2048]{2,1,0:T(8,128)(2,1)} copy(bf16[4,256,2048]{1,2,0:T(8,128)(2,1)} %bitcast.1) | data formatting | bytes 8388608 | tf_op jit(solution)/shard_map/all_to_all | solution.py:20
  101.6 0.0 copy-start
  101.6 23.7 %convolution_convert_fusion.1 = bf16[1024,3584]{1,0:T(8,128)(2,1)} fusion(bf16[1024,2048]{1,0:T(8,128)(2,1)} %bitcast.35, bf16[2048,3584]{0,1:T(8,128)(2,1)} %get-tuple-element.5), kind=kOutput, calls=%fused_computation.20 | convolution fusion | flops 15036055552 | bytes 26214400 | tf_op jit(solution)/shard_map/dot_general | solution.py:27
  125.3 0.0 copy-done
  125.3 20.5 %convolution_convert_fusion = bf16[1024,3584]{1,0:T(8,128)(2,1)} fusion(bf16[1024,2048]{1,0:T(8,128)(2,1)S(1)} %bitcast.36, bf16[2048,3584]{0,1:T(8,128)(2,1)} %get-tuple-element.6), kind=kOutput, calls=%fused_computation.19 | convolution fusion | flops 15036055552 | bytes 26214400 | tf_op jit(solution)/shard_map/dot_general | solution.py:28
  145.8 12.6 %pad_maximum_fusion = bf16[1024,7168]{1,0:T(8,128)(2,1)} fusion(bf16[1024,3584]{1,0:T(8,128)(2,1)} %convolution_convert_fusion, bf16[1024,3584]{1,0:T(8,128)(2,1)} %convolution_convert_fusion.1), kind=kLoop, calls=%fused_computation.12 | loop fusion | flops 29360128 | bytes 29360128 | tf_op jit(solution)/shard_map/concatenate | solution.py:30
  158.4 0.0 reduce-scatter.3.cloned.1.call-update
  158.5 0.0 all-gather.2.cloned.1.call-start
  158.5 117.2 %reduce-scatter.3.cloned.1.call-done = bf16[256,7168]{1,0:T(8,128)(2,1)} async-done(((bf16[1024,7168]{1,0:T(8,128)(2,1)}), bf16[256,7168]{1,0:T(8,128)(2,1)}) %reduce-scatter.3.cloned.1.call-update) | async-done | bytes 3670032 | tf_op jit(solution)/shard_map/reduce_scatter | solution.py:29
  275.7 2.9 convert_element_type.25
  278.6 2.5 multiply_reduce_fusion.1
  281.2 0.0 all-gather.2.cloned.1.call-update
  281.2 0.0 reduce-scatter.5.cloned.1.call-start
  281.2 0.1 shift_right_arithmetic.72
  281.3 0.0 copy-start.3
  281.3 19.5 %copy.21 = bf16[3584,2048]{0,1:T(8,128)(2,1)} copy(bf16[3584,2048]{1,0:T(8,128)(2,1)} %param.14) | data formatting | bytes 29360128 | tf_op args[6]
  300.8 0.0 copy-done.3
  300.8 15.1 %fusion.8 = bf16[3584,2048]{0,1:T(8,128)(2,1)} fusion(bf16[3584,2048]{0,1:T(8,128)(2,1)} %copy.21, s32[2048]{0:T(1024)S(1)} %shift_right_arithmetic.72, s32[3584,64]{0,1:T(8,128)S(1)} %copy-done.3), kind=kLoop, calls=%fused_computation.11 | loop fusion | flops 29360128 | bytes 30285824 | tf_op jit(solution)/shard_map/jit(_where)/select_n | solution.py:11
  315.9 17.7 %all-gather.2.cloned.1.call-done = bf16[1024,3584]{1,0:T(8,128)(2,1)} async-done(((bf16[256,3584]{1,0:T(8,128)(2,1)}), bf16[1024,3584]{1,0:T(8,128)(2,1)}) %all-gather.2.cloned.1.call-update) | async-done | bytes 7340048 | tf_op jit(solution)/shard_map/all_gather | solution.py:40
  333.6 21.2 %convolution_convert_fusion.2 = bf16[1024,2048]{1,0:T(8,128)(2,1)} fusion(bf16[1024,3584]{1,0:T(8,128)(2,1)} %all-gather.2.cloned.1.call-done, bf16[3584,2048]{0,1:T(8,128)(2,1)} %fusion.8), kind=kOutput, calls=%fused_computation.21 | convolution fusion | flops 15034482688 | bytes 26214400 | tf_op jit(solution)/shard_map/dot_general | solution.py:39
  354.8 0.0 reduce-scatter.5.cloned.1.call-update
  354.9 3.1 multiply_reduce_fusion
  357.9 0.6 sqrt.6
  358.6 10.6 %psum.7 = f32[3584]{0:T(1024)S(1)} all-reduce(f32[3584]{0:T(1024)S(1)} %get-tuple-element.3), channel_id=1, replica_groups=mesh['dp'=4,'mp'=8] {'dp'}, use_global_device_ids=true, to_apply=%region_5.6 | all-reduce | flops 3584 | bytes 28672 | tf_op jit(solution)/shard_map/psum | solution.py:37
  369.2 0.6 sqrt.7
  369.8 73.5 %reduce-scatter.5.cloned.1.call-done = bf16[128,2048]{1,0:T(8,128)(2,1)} async-done(((bf16[1024,2048]{1,0:T(8,128)(2,1)}), bf16[128,2048]{1,0:T(8,128)(2,1)}) %reduce-scatter.5.cloned.1.call-update) | async-done | bytes 524304 | tf_op jit(solution)/shard_map/reduce_scatter | solution.py:44
  (3 shorter events, 0.0 us)
Async XLA Ops:
  7.2 9.7 %copy-start.4 = (f32[8192]{0:T(1024)S(1)}, f32[8192]{0:T(1024)}, u32[]{:S(2)}) copy-start(f32[8192]{0:T(1024)} %param.9) | copy-start | bytes 98308
  21.0 74.2 %all-to-all-start = ((bf16[256,4,2048]{0,2,1:T(8,128)(2,1)}), bf16[256,4,2048]{0,2,1:T(8,128)(2,1)}, u32[]{:S(2)}, u32[]{:S(2)}) async-start(bf16[256,4,2048]{0,2,1:T(8,128)(2,1)} %bitcast.34), calls=%async_computation | async-start | bytes 8388608 | tf_op jit(solution)/shard_map/all_to_all | solution.py:20
  25.9 249.8 %reduce-scatter.3.cloned.1.call-start = ((), (), s32[]{:S(2)}) async-start(), calls=%async_computation.3 | async-start | bytes 18350080 | tf_op jit(solution)/shard_map/reduce_scatter | solution.py:29
  46.4 20.5 %copy-start.1 = (s32[2048,112]{0,1:T(8,128)S(1)}, s32[2048,112]{0,1:T(8,128)}, u32[]{:S(2)}) copy-start(s32[2048,112]{0,1:T(8,128)} %param.11) | copy-start | bytes 2752516
  46.4 20.5 %copy-start.2 = (s32[2048,112]{0,1:T(8,128)S(1)}, s32[2048,112]{0,1:T(8,128)}, u32[]{:S(2)}) copy-start(s32[2048,112]{0,1:T(8,128)} %param.13) | copy-start | bytes 2752516
  101.6 23.7 %copy-start = (bf16[4,256,2048]{2,1,0:T(8,128)(2,1)S(1)}, bf16[4,256,2048]{2,1,0:T(8,128)(2,1)}, u32[]{:S(2)}) copy-start(bf16[4,256,2048]{2,1,0:T(8,128)(2,1)} %copy.18) | copy-start | bytes 12582916
  158.5 175.2 %all-gather.2.cloned.1.call-start = ((), (), s32[]{:S(2)}) async-start(), calls=%async_computation.4 | async-start | bytes 9175040 | tf_op jit(solution)/shard_map/all_gather | solution.py:40
  281.2 162.1 %reduce-scatter.5.cloned.1.call-start = ((), (), s32[]{:S(2)}) async-start(), calls=%async_computation.5 | async-start | bytes 4718592 | tf_op jit(solution)/shard_map/reduce_scatter | solution.py:44
  281.3 19.5 %copy-start.3 = (s32[3584,64]{0,1:T(8,128)S(1)}, s32[3584,64]{0,1:T(8,128)}, u32[]{:S(2)}) copy-start(s32[3584,64]{0,1:T(8,128)} %param.15) | copy-start | bytes 2752516
Sparse Core Ops, SparseCore 0:
  158.6 117.0 reduce-scatter.2
  281.3 52.2 all-gather.1
  355.0 88.2 reduce-scatter.4
where the time goes:
time: 452 us; the launch traced here: 450 us
  waiting for transfers between devices  208 us (46%)
  local copies, waits for them, and re-layouts  74.5 us (16%)
  other arithmetic  72 us (16%)
  matrix products  65.4 us (14%)
  between operations  13.8 us (3%)
  blocking collectives  10.6 us (2%)
  starting transfers between devices  5.01 us (1%)
    reduce_scatter x1, waiting for transfers between devices, on_device(): lax.psum_scatter(jnp.concatenate([gate_part, up_part], axis=1).astype(jnp...  117 us
    reduce_scatter x1, waiting for transfers between devices, on_device(): lax.psum_scatter(partial_out.astype(jnp.bfloat16), 'mp', scatter_dimensio...  73.5 us
    unnamed x14, local copies, waits for them, and re-layouts  66.7 us
    select_n x2, other arithmetic, keep_entries(): return jnp.where(kept_bits == 1, weight, jnp.zeros_like(weight))  43.5 us
    dot_general x1, matrix products, on_device(): gate_part = jnp.dot(columns, gate_kept, preferred_element_type=jnp.float32)  23.7 us
    dot_general x1, matrix products, on_device(): jnp.dot(lax.all_gather(hidden, 'dp', axis=0, tiled=True), down_kept, pref...  21.2 us
    dot_general x1, matrix products, on_device(): up_part = jnp.dot(columns, up_kept, preferred_element_type=jnp.float32)  20.5 us
    all_gather x1, waiting for transfers between devices, on_device(): lax.all_gather(hidden, 'dp', axis=0, tiled=True)  17.7 us
  transfers between devices with their start and end apart: 4, of which 3 were waited for; matrix products, arithmetic and copies ran while one was open for 24% of the time, Pallas kernels for 0%

commit v1 on v0

--- a/solution.py
+++ b/solution.py
@@ -2,6 +2,13 @@
 import jax.numpy as jnp
 from jax import lax
 from jax.sharding import PartitionSpec as P
+
+
+def exchange_blocks(shard, axis, split, join):
+    size = lax.axis_size(axis)
+    blocks = jnp.stack(jnp.split(shard, size, axis=split), axis=0)
+    blocks = lax.all_to_all(blocks, axis, split_axis=0, concat_axis=0)
+    return jnp.concatenate(blocks, axis=join)
 
 
 def keep_entries(weight, packed):
@@ -17,7 +24,7 @@
     values = tokens.astype(jnp.float32)
     scale = lax.rsqrt(jnp.mean(values * values, axis=1, keepdims=True) + 1e-05)
     normed = (values * scale * norm_gain).astype(jnp.bfloat16)
-    columns = lax.all_to_all(normed, "dp", split_axis=1, concat_axis=0, tiled=True)
+    columns = exchange_blocks(normed, "dp", 1, 0)
     widened = columns.astype(jnp.float32)
     input_norms = jnp.sqrt(jnp.sum(widened * widened, axis=0))
     gate_kept = keep_entries(gate_weight, gate_mask)

time: 452 us -> 440 us (0.973)
  local copies, waits for them, and re-layouts: 74.5 us -> 62.2 us
    unnamed x14 -> x9, local copies, waits for them, and re-layouts: 66.7 us -> 60.3 us
    all_to_all x1 -> x0, local copies, waits for them, and re-layouts: 6.33 us -> none  [on_device(): lax.all_to_all(normed, 'dp', split_axis=1, concat_axis=0, tiled=True)]
  transfers between devices with their start and end apart: 4 -> 4, of which waited for: 3 -> 3; matrix products, arithmetic and copies ran while one was open for 24% -> 25% of each run, Pallas kernels for 0% -> 0%
where the time goes in v1:
time: 440 us; the launch traced here: 438 us
  waiting for transfers between devices  208 us (47%)
  other arithmetic  73.5 us (17%)
  matrix products  64.7 us (15%)
  local copies, waits for them, and re-layouts  62.2 us (14%)
  between operations  13.8 us (3%)
  blocking collectives  10.6 us (2%)
  starting transfers between devices  5.01 us (1%)
    reduce_scatter x1, waiting for transfers between devices, on_device(): lax.psum_scatter(jnp.concatenate([gate_part, up_part], axis=1).astype(jnp...  117 us
    reduce_scatter x1, waiting for transfers between devices, on_device(): lax.psum_scatter(partial_out.astype(jnp.bfloat16), 'mp', scatter_dimensio...  73.5 us
    unnamed x9, local copies, waits for them, and re-layouts  60.3 us
    select_n x2, other arithmetic, keep_entries(): return jnp.where(kept_bits == 1, weight, jnp.zeros_like(weight))  43.4 us
    dot_general x1, matrix products, on_device(): gate_part = jnp.dot(columns, gate_kept, preferred_element_type=jnp.float32)  21.8 us
    dot_general x1, matrix products, on_device(): up_part = jnp.dot(columns, up_kept, preferred_element_type=jnp.float32)  21.7 us
    dot_general x1, matrix products, on_device(): jnp.dot(lax.all_gather(hidden, 'dp', axis=0, tiled=True), down_kept, pref...  21.2 us
    all_gather x1, waiting for transfers between devices, on_device(): lax.all_gather(hidden, 'dp', axis=0, tiled=True)  17.7 us
  transfers between devices with their start and end apart: 4, of which 3 were waited for; matrix products, arithmetic and copies ran while one was open for 25% of the time, Pallas kernels for 0%

profile of v1, /device:TPU:0, one launch (start us, length us, event | category | flops | bytes accessed | tf_op | source)
XLA Modules:
  0.0 438.3 jit_solution(2331683268427819935)
XLA Ops:
  7.2 3.1 fusion.9
  10.3 3.6 fusion.11
  13.9 0.5 slice_bitcast_fusion.3
  14.4 2.2 pad_maximum_fusion.1
  16.6 4.9 %all-to-all-start = ((bf16[4,256,2048]{2,1,0:T(8,128)(2,1)}), bf16[4,256,2048]{2,1,0:T(8,128)(2,1)}, u32[]{:S(2)}, u32[]{:S(2)}) async-start(bf16[4,256,2048]{2,1,0:T(8,128)(2,1)} %pad_maximum_fusion.1), calls=%async_computation | async-start | bytes 8388608 | tf_op jit(solution)/shard_map/all_to_all | solution.py:10
  21.5 0.0 reduce-scatter.3.cloned.1.call-start
  21.6 20.2 %copy.14 = bf16[2048,3584]{0,1:T(8,128)(2,1)} copy(bf16[2048,3584]{1,0:T(8,128)(2,1)} %param.10) | data formatting | bytes 29360128 | tf_op args[2]
  41.8 0.0 copy-start
  41.8 0.0 copy-start.1
  41.8 20.5 %copy.15 = bf16[2048,3584]{0,1:T(8,128)(2,1)} copy(bf16[2048,3584]{1,0:T(8,128)(2,1)} %param.12) | data formatting | bytes 29360128 | tf_op args[4]
  62.3 0.1 shift_right_arithmetic.63
  62.4 0.0 copy-done
  62.4 0.0 copy-done.1
  62.4 28.3 %fusion.6 = (bf16[2048,3584]{0,1:T(8,128)(2,1)}, bf16[2048,3584]{0,1:T(8,128)(2,1)}) fusion(bf16[2048,3584]{0,1:T(8,128)(2,1)} %copy.14, s32[3584]{0:T(1024)S(1)} %shift_right_arithmetic.63, s32[2048,112]{0,1:T(8,128)S(1)} %copy-done, bf16[2048,3584]{0,1:T(8,128)(2,1)} %copy.15, s32[2048,112]{0,1:T(8,128)S(1)} %copy-done.1), kind=kLoop, calls=%fused_computation.9 | loop fusion | flops 58720256 | bytes 60569600 | tf_op jit(solution)/shard_map/jit(_where)/select_n | solution.py:18
  90.8 0.0 all-to-all-done
  90.8 21.7 %convolution_convert_fusion = bf16[1024,3584]{1,0:T(8,128)(2,1)} fusion(bf16[1024,2048]{1,0:T(8,128)(2,1)} %bitcast.4, bf16[2048,3584]{0,1:T(8,128)(2,1)} %get-tuple-element.10), kind=kOutput, calls=%fused_computation.19 | convolution fusion | flops 15036055552 | bytes 26214400 | tf_op jit(solution)/shard_map/dot_general | solution.py:35
  112.5 21.8 %convolution_convert_fusion.1 = bf16[1024,3584]{1,0:T(8,128)(2,1)} fusion(bf16[1024,2048]{1,0:T(8,128)(2,1)} %bitcast.4, bf16[2048,3584]{0,1:T(8,128)(2,1)} %get-tuple-element.9), kind=kOutput, calls=%fused_computation.20 | convolution fusion | flops 15036055552 | bytes 26214400 | tf_op jit(solution)/shard_map/dot_general | solution.py:34
  134.3 12.6 %pad_maximum_fusion = bf16[1024,7168]{1,0:T(8,128)(2,1)} fusion(bf16[1024,3584]{1,0:T(8,128)(2,1)} %convolution_convert_fusion, bf16[1024,3584]{1,0:T(8,128)(2,1)} %convolution_convert_fusion.1), kind=kLoop, calls=%fused_computation.12 | loop fusion | flops 29360128 | bytes 29360128 | tf_op jit(solution)/shard_map/concatenate | solution.py:37
  146.9 0.0 reduce-scatter.3.cloned.1.call-update
  147.0 0.0 all-gather.2.cloned.1.call-start
  147.0 117.2 %reduce-scatter.3.cloned.1.call-done = bf16[256,7168]{1,0:T(8,128)(2,1)} async-done(((bf16[1024,7168]{1,0:T(8,128)(2,1)}), bf16[256,7168]{1,0:T(8,128)(2,1)}) %reduce-scatter.3.cloned.1.call-update) | async-done | bytes 3670032 | tf_op jit(solution)/shard_map/reduce_scatter | solution.py:36
  264.2 2.9 convert_element_type.25
  267.1 2.5 multiply_reduce_fusion.1
  269.6 0.0 all-gather.2.cloned.1.call-update
  269.7 0.0 copy-start.2
  269.7 0.0 reduce-scatter.5.cloned.1.call-start
  269.7 19.5 %copy.16 = bf16[3584,2048]{0,1:T(8,128)(2,1)} copy(bf16[3584,2048]{1,0:T(8,128)(2,1)} %param.14) | data formatting | bytes 29360128 | tf_op args[6]
  289.3 0.1 shift_right_arithmetic.72
  289.3 0.0 copy-done.2
  289.3 15.1 %fusion.8 = bf16[3584,2048]{0,1:T(8,128)(2,1)} fusion(bf16[3584,2048]{0,1:T(8,128)(2,1)} %copy.16, s32[2048]{0:T(1024)S(1)} %shift_right_arithmetic.72, s32[3584,64]{0,1:T(8,128)S(1)} %copy-done.2), kind=kLoop, calls=%fused_computation.11 | loop fusion | flops 29360128 | bytes 30285824 | tf_op jit(solution)/shard_map/jit(_where)/select_n | solution.py:18
  304.4 17.7 %all-gather.2.cloned.1.call-done = bf16[1024,3584]{1,0:T(8,128)(2,1)} async-done(((bf16[256,3584]{1,0:T(8,128)(2,1)}), bf16[1024,3584]{1,0:T(8,128)(2,1)}) %all-gather.2.cloned.1.call-update) | async-done | bytes 7340048 | tf_op jit(solution)/shard_map/all_gather | solution.py:47
  322.1 21.2 %convolution_convert_fusion.2 = bf16[1024,2048]{1,0:T(8,128)(2,1)} fusion(bf16[1024,3584]{1,0:T(8,128)(2,1)} %all-gather.2.cloned.1.call-done, bf16[3584,2048]{0,1:T(8,128)(2,1)} %fusion.8), kind=kOutput, calls=%fused_computation.22 | convolution fusion | flops 15034482688 | bytes 26214400 | tf_op jit(solution)/shard_map/dot_general | solution.py:46
  343.3 0.0 reduce-scatter.5.cloned.1.call-update
  343.4 3.1 multiply_reduce_fusion
  346.4 0.6 sqrt.6
  347.1 10.6 %psum.7 = f32[3584]{0:T(1024)S(1)} all-reduce(f32[3584]{0:T(1024)S(1)} %get-tuple-element.3), channel_id=1, replica_groups=mesh['dp'=4,'mp'=8] {'dp'}, use_global_device_ids=true, to_apply=%region_5.6 | all-reduce | flops 3584 | bytes 28672 | tf_op jit(solution)/shard_map/psum | solution.py:44
  357.7 0.6 sqrt.7
  358.3 73.5 %reduce-scatter.5.cloned.1.call-done = bf16[128,2048]{1,0:T(8,128)(2,1)} async-done(((bf16[1024,2048]{1,0:T(8,128)(2,1)}), bf16[128,2048]{1,0:T(8,128)(2,1)}) %reduce-scatter.5.cloned.1.call-update) | async-done | bytes 524304 | tf_op jit(solution)/shard_map/reduce_scatter | solution.py:51
  (3 shorter events, 0.0 us)
Async XLA Ops:
  16.6 74.1 %all-to-all-start = ((bf16[4,256,2048]{2,1,0:T(8,128)(2,1)}), bf16[4,256,2048]{2,1,0:T(8,128)(2,1)}, u32[]{:S(2)}, u32[]{:S(2)}) async-start(bf16[4,256,2048]{2,1,0:T(8,128)(2,1)} %pad_maximum_fusion.1), calls=%async_computation | async-start | bytes 8388608 | tf_op jit(solution)/shard_map/all_to_all | solution.py:10
  21.5 242.7 %reduce-scatter.3.cloned.1.call-start = ((), (), s32[]{:S(2)}) async-start(), calls=%async_computation.3 | async-start | bytes 18350080 | tf_op jit(solution)/shard_map/reduce_scatter | solution.py:36
  41.8 20.6 %copy-start = (s32[2048,112]{0,1:T(8,128)S(1)}, s32[2048,112]{0,1:T(8,128)}, u32[]{:S(2)}) copy-start(s32[2048,112]{0,1:T(8,128)} %param.11) | copy-start | bytes 2752516
  41.8 20.6 %copy-start.1 = (s32[2048,112]{0,1:T(8,128)S(1)}, s32[2048,112]{0,1:T(8,128)}, u32[]{:S(2)}) copy-start(s32[2048,112]{0,1:T(8,128)} %param.13) | copy-start | bytes 2752516
  147.0 175.2 %all-gather.2.cloned.1.call-start = ((), (), s32[]{:S(2)}) async-start(), calls=%async_computation.4 | async-start | bytes 9175040 | tf_op jit(solution)/shard_map/all_gather | solution.py:47
  269.7 19.7 %copy-start.2 = (s32[3584,64]{0,1:T(8,128)S(1)}, s32[3584,64]{0,1:T(8,128)}, u32[]{:S(2)}) copy-start(s32[3584,64]{0,1:T(8,128)} %param.15) | copy-start | bytes 2752516
  269.7 162.1 %reduce-scatter.5.cloned.1.call-start = ((), (), s32[]{:S(2)}) async-start(), calls=%async_computation.5 | async-start | bytes 4718592 | tf_op jit(solution)/shard_map/reduce_scatter | solution.py:51
Sparse Core Ops, SparseCore 0:
  147.1 117.0 reduce-scatter.2
  269.8 52.2 all-gather.1
  343.5 88.2 reduce-scatter.4
